TPU v7x, 32 devices: a whole 2x2x4 slice. The times are simulated.
32 devices in a mesh: aa: 4 (over z), ba: 8 (over y, x, core).
Axes of the slice: x: 2, y: 2, z: 4, core: 2. Of those that a mesh axis runs over, the one named last changes fastest.
Arguments:
- grad_out: bfloat16 [4096, 4096], P('aa', 'ba')
- saved_input: bfloat16 [4096, 4096], P(('aa', 'ba'))
- keep_bits: int32 [4096, 128], P(('aa', 'ba')), may hold values from -2147483648 to 2147483647, as said below
- gain: float32 [4096], replicated, may hold values from 0.5 to 1.5
Outputs:
- grad_in: bfloat16 [4096, 4096], P(('aa', 'ba'))
- gain_grad: float32 [4096], P('ba')
Inputs may be any that keep to these rules, and one draw needn't show every extreme that they name: `keep_bits`: bit k of word w in row t (bit 31 being the sign bit) is the keep flag of feature 32 * w + k of token t; about nine in ten flags are 1.
All inputs are finite; a program needn't handle non-finite values.
Results may differ from a plain program's by a relative error of at most 0.001.
Values may be sent and summed in bfloat16 or wider, within the bound.
A program may use at most 64 MiB of HBM per device.

v0:
```python
import functools
import math

import jax
import jax.numpy as jnp
from jax import lax
from jax.experimental import pallas as pl
from jax.experimental.pallas import tpu as pltpu
from jax.sharding import PartitionSpec as P

KEEP_RATE = 0.9
EPSILON = 1e-06
LANES = 128
CHUNK_ROWS = 64
STORES = 4
MESH = pl.DeviceIdType.MESH


def unpack_bits(words):
    shifts = jnp.arange(32, dtype=jnp.int32)
    bits = jnp.right_shift(words[:, :, None], shifts[None, None, :]) & 1
    return bits.reshape(words.shape[0], words.shape[1] * 32).astype(jnp.float32)


def rows_backward(grad_rows, input_rows, word_rows, gain):
    keep = unpack_bits(word_rows)
    dropped = input_rows.astype(jnp.float32) * keep * (1.0 / KEEP_RATE)
    inverse = lax.rsqrt(jnp.mean(dropped * dropped, axis=-1, keepdims=True) + EPSILON)
    normed = dropped * inverse
    grads = grad_rows.astype(jnp.float32)
    scaled = gain[None, :] * grads
    centre = jnp.mean(scaled * normed, axis=-1, keepdims=True)
    grad_in = (inverse * (scaled - normed * centre) * keep * (1.0 / KEEP_RATE)).astype(jnp.bfloat16)
    partial_sum = jnp.sum(grads * normed, axis=0)
    return (grad_in, partial_sum)


def plain(grad_out, saved_input, keep_bits, gain):
    groups = lax.axis_size("ba")
    rows = grad_out.shape[0] // groups
    pieces = grad_out.reshape(groups, rows, grad_out.shape[1])
    arrived = lax.all_to_all(pieces, "ba", split_axis=0, concat_axis=2, tiled=True)
    grad_rows = arrived.reshape(rows, arrived.shape[2])
    grad_in, partial_sum = rows_backward(grad_rows, saved_input, keep_bits, gain)
    total_tokens = rows * groups * lax.axis_size("aa")
    owned = lax.psum_scatter(partial_sum, "ba", scatter_dimension=0, tiled=True)
    share = lax.psum(owned, "aa")
    gain_grad = share * (1.0 / math.sqrt(total_tokens))
    return (grad_in, gain_grad)


def late_steps(n_ba):
    return list(range(max(1, n_ba // 4), n_ba - n_ba // 4))


def kernel(n_ba, n_aa, grad_hbm, input_hbm, bits_hbm, gain_hbm, out_ref, share_ref,
           staged, arrived, held, words, gain_ref, normed, masked_gain, outer, totals, sums,
           parts, slices, shares, far_shares, stage_sem, load_sem, near_send, near_recv,
           far_send, far_recv, part_send, part_recv, share_send, share_recv,
           late_send, late_recv, ready):
    ba, aa = lax.axis_index("ba"), lax.axis_index("aa")
    rows, width = arrived.shape[1], arrived.shape[2]
    depth = n_ba * width
    chunks = rows // CHUNK_ROWS
    tiles = width // LANES
    far = late_steps(n_ba)
    far = sorted(far, key=lambda step: step % 2)
    n_far = len(far)
    near = [step for step in range(1, n_ba) if step not in far]
    near_order = sorted(near, reverse=True)

    def column(step):
        return lax.rem(aa + step, n_aa)

    def column_source(step):
        return lax.rem(aa + n_aa - step, n_aa)

    def rows_of(chunk):
        start = chunk * CHUNK_ROWS
        if not isinstance(start, int):
            start = pl.multiple_of(start, CHUNK_ROWS)
        return pl.ds(start, CHUNK_ROWS)

    def stage(step):
        first = pl.ds(pl.multiple_of((ba ^ step) * rows, CHUNK_ROWS), rows)
        target = staged.at[step] if step else arrived.at[0]
        return pltpu.make_async_copy(grad_hbm.at[first], target, stage_sem.at[step])

    def near_piece(step):
        return pltpu.make_async_remote_copy(
            src_ref=staged.at[step], dst_ref=arrived.at[step],
            send_sem=near_send.at[step], recv_sem=near_recv.at[step],
            device_id={"ba": ba ^ step}, device_id_type=MESH,
        )

    def far_piece(chunk, index):
        step, block = far[index], rows_of(chunk)
        return pltpu.make_async_remote_copy(
            src_ref=staged.at[step, block], dst_ref=arrived.at[step, block],
            send_sem=far_send.at[chunk, index], recv_sem=far_recv.at[chunk, index],
            device_id={"ba": ba ^ step}, device_id_type=MESH,
        )

    def part(step):
        return pltpu.make_async_remote_copy(
            src_ref=parts.at[step], dst_ref=slices.at[step],
            send_sem=part_send.at[step], recv_sem=part_recv.at[step],
            device_id={"ba": ba ^ step}, device_id_type=MESH,
        )

    def share(step, slot):
        return pltpu.make_async_remote_copy(
            src_ref=shares.at[aa], dst_ref=shares.at[slot],
            send_sem=share_send.at[step], recv_sem=share_recv.at[step],
            device_id={"aa": column(step)}, device_id_type=MESH,
        )

    def late(step, index, slot):
        return pltpu.make_async_remote_copy(
            src_ref=parts.at[far[index]], dst_ref=far_shares.at[slot, index],
            send_sem=late_send.at[step, index], recv_sem=late_recv.at[step, index],
            device_id={"aa": column(step), "ba": ba ^ far[index]}, device_id_type=MESH,
        )

    barrier = pltpu.get_barrier_semaphore()
    for step in range(1, n_ba):
        pl.semaphore_signal(barrier, inc=1, device_id={"ba": ba ^ step}, device_id_type=MESH)
    for step in range(1, n_aa):
        pl.semaphore_signal(barrier, inc=1, device_id={"aa": column(step)}, device_id_type=MESH)
    for step in near_order:
        stage(step).start()
    loads = [
        pltpu.make_async_copy(bits_hbm, words, load_sem.at[0]),
        pltpu.make_async_copy(gain_hbm, gain_ref, load_sem.at[1]),
        pltpu.make_async_copy(input_hbm, held, load_sem.at[2]),
    ]
    for load in loads:
        load.start()
    for step in far + [0]:
        stage(step).start()
    pl.semaphore_wait(barrier, n_ba + n_aa - 2)
    for step in near_order:
        stage(step).wait()
        near_piece(step).start()
    for step in far:
        pl.semaphore_signal(ready, inc=1, device_id={"ba": ba ^ step}, device_id_type=MESH)
        stage(step).wait()
    for load in loads:
        load.wait()

    lane = lax.broadcasted_iota(jnp.int32, (CHUNK_ROWS, LANES), 1)
    word_of = lane // 32
    flag = jnp.left_shift(jnp.int32(1), lane % 32)

    def span(source, tile):
        return pl.ds(pl.multiple_of(source * width + tile * LANES, LANES), LANES)

    def prepare(chunk, carry):
        block = rows_of(chunk)

        def drop(source, squares):
            row_words = words[block, :]
            for tile in range(tiles):
                at = span(source, tile)
                index = word_of + (source * tiles + tile) * (LANES // 32)
                spread = jnp.take_along_axis(row_words, index, axis=1, mode="promise_in_bounds")
                kept = (spread & flag) != 0
                dropped = jnp.where(kept, held[block, at].astype(jnp.float32), 0.0) * (1.0 / KEEP_RATE)
                normed[block, at] = dropped
                masked_gain[block, at] = jnp.where(kept, gain_ref[:, at], 0.0)
                squares = squares + dropped * dropped
            return squares

        squares = lax.fori_loop(0, n_ba, drop, jnp.zeros((CHUNK_ROWS, LANES), jnp.float32))
        mean = jnp.sum(squares, axis=1, keepdims=True) * (1.0 / depth)
        inverse = lax.rsqrt(mean + EPSILON)
        outer[block, :] = jnp.broadcast_to(inverse * (1.0 / KEEP_RATE), (CHUNK_ROWS, LANES))

        def scale(source, none):
            for tile in range(tiles):
                at = span(source, tile)
                normed[block, at] = normed[block, at] * inverse
            return none

        lax.fori_loop(0, n_ba, scale, 0)
        return carry

    lax.fori_loop(0, chunks, prepare, 0)
    sums[...] = jnp.zeros_like(sums)
    totals[...] = jnp.zeros_like(totals)
    for step in near:
        near_piece(step).wait_send()
    ahead = chunks // 2
    for chunk in range(ahead):
        for index in range(n_far):
            far_piece(chunk, index).start()

    def first(step, chunk):
        block, source = rows_of(chunk), ba ^ step
        total = totals[block, :]
        for tile in range(tiles):
            at = span(source, tile)
            here = slice(tile * LANES, (tile + 1) * LANES)
            grads = arrived[step, block, here].astype(jnp.float32)
            product = grads * normed[block, at]
            total = total + product * gain_ref[:, at]
            sums[step, :, here] += jnp.sum(product.reshape(CHUNK_ROWS // 8, 8, LANES), axis=0)
        totals[block, :] = total

    def finish(chunk):
        block = rows_of(chunk)
        factor = outer[block, :]
        centre = jnp.sum(totals[block, :], axis=1, keepdims=True) * (1.0 / depth)

        def last(step, none):
            for tile in range(tiles):
                at = span(ba ^ step, tile)
                grads = arrived[step, block, tile * LANES:(tile + 1) * LANES].astype(jnp.float32)
                value = factor * (masked_gain[block, at] * grads - normed[block, at] * centre)
                out_ref[block, at] = value.astype(jnp.bfloat16)
            return none

        lax.fori_loop(0, n_ba, last, 0)

    def fold(step):
        return jnp.sum(sums[step], axis=0, keepdims=True)

    for step in [0] + near:
        if step:
            near_piece(step).wait_recv()
        else:
            stage(0).wait()

        def whole(chunk, none, step=step):
            first(step, chunk)
            return none

        lax.fori_loop(0, chunks, whole, 0)
        if step:
            parts[step] = fold(step)
        else:
            slices[0] = fold(0)
    for step in reversed(near):
        part(step).start()
    for chunk in range(ahead, chunks):
        for index in range(n_far):
            far_piece(chunk, index).start()

    def gather_near():
        total = slices[0]
        for step in near:
            part(step).wait_recv()
            total = total + slices[step]
        shares[aa] = total
        for step in range(1, n_aa):
            share(step, aa).start()

    for chunk in range(chunks):
        if chunk == chunks - 1:
            gather_near()
        for index in range(n_far):
            far_piece(chunk, index).wait_recv()
            first(far[index], chunk)
        if chunk < chunks - 1:
            finish(chunk)
    for step in far:
        parts[step] = fold(step)
    pl.semaphore_wait(ready, n_far)
    for step in reversed(range(n_aa)):
        for index in range(n_far):
            late(step, index, aa).start()
    finish(chunks - 1)
    for step in near:
        part(step).wait_send()
    for chunk in range(chunks):
        for index in range(n_far):
            far_piece(chunk, index).wait_send()
    for step in range(1, n_aa):
        share(step, column_source(step)).wait_recv()
    for step in range(n_aa):
        for index in range(n_far):
            late(step, index, column_source(step)).wait_recv()
    total = jnp.zeros((1, width), jnp.float32)
    for source in range(n_aa):
        total = total + shares[source]
        for index in range(n_far):
            total = total + far_shares[source, index]
    share_ref[...] = total * (1.0 / math.sqrt(rows * n_ba * n_aa))
    for step in range(1, n_aa):
        share(step, aa).wait_send()
    for step in range(n_aa):
        for index in range(n_far):
            late(step, index, aa).wait_send()


def store(grad_vmem, share_vmem, grad_hbm, share_hbm, sem):
    rows = grad_vmem.shape[0] // STORES
    copies = [pltpu.make_async_copy(share_vmem, share_hbm, sem.at[STORES])]
    for index in range(STORES):
        block = pl.ds(index * rows, rows)
        copies.append(pltpu.make_async_copy(grad_vmem.at[block], grad_hbm.at[block], sem.at[index]))
    for copy in copies:
        copy.start()
    for copy in copies:
        copy.wait()


def fused(grad_out, saved_input, keep_bits, gain):
    n_ba, n_aa = lax.axis_size("ba"), lax.axis_size("aa")
    width = grad_out.shape[1]
    rows, depth = saved_input.shape
    chunks, n_far = rows // CHUNK_ROWS, len(late_steps(n_ba))
    f32 = jnp.float32
    grad_in, share = pl.pallas_call(
        functools.partial(kernel, n_ba, n_aa),
        out_shape=(
            pltpu.VMEM((rows, depth), jnp.bfloat16),
            pltpu.VMEM((1, width), f32),
        ),
        in_specs=[pl.BlockSpec(memory_space=pl.ANY)] * 4,
        out_specs=(pl.BlockSpec(memory_space=pltpu.VMEM), pl.BlockSpec(memory_space=pltpu.VMEM)),
        scratch_shapes=[
            pltpu.VMEM((n_ba, rows, width), jnp.bfloat16),
            pltpu.VMEM((n_ba, rows, width), jnp.bfloat16),
            pltpu.VMEM((rows, depth), jnp.bfloat16),
            pltpu.VMEM(keep_bits.shape, jnp.int32),
            pltpu.VMEM((1, depth), f32),
            pltpu.VMEM((rows, depth), f32),
            pltpu.VMEM((rows, depth), f32),
            pltpu.VMEM((rows, LANES), f32),
            pltpu.VMEM((rows, LANES), f32),
            pltpu.VMEM((n_ba, 8, width), f32),
            pltpu.VMEM((n_ba, 1, width), f32),
            pltpu.VMEM((n_ba, 1, width), f32),
            pltpu.VMEM((n_aa, 1, width), f32),
            pltpu.VMEM((n_aa, n_far, 1, width), f32),
            pltpu.SemaphoreType.DMA((n_ba,)),
            pltpu.SemaphoreType.DMA((3,)),
            pltpu.SemaphoreType.DMA((n_ba,)),
            pltpu.SemaphoreType.DMA((n_ba,)),
            pltpu.SemaphoreType.DMA((chunks, n_far)),
            pltpu.SemaphoreType.DMA((chunks, n_far)),
            pltpu.SemaphoreType.DMA((n_ba,)),
            pltpu.SemaphoreType.DMA((n_ba,)),
            pltpu.SemaphoreType.DMA((n_aa,)),
            pltpu.SemaphoreType.DMA((n_aa,)),
            pltpu.SemaphoreType.DMA((n_aa, n_far)),
            pltpu.SemaphoreType.DMA((n_aa, n_far)),
            pltpu.SemaphoreType.REGULAR,
        ],
        compiler_params=pltpu.CompilerParams(collective_id=0, has_side_effects=True),
        name="regroup_backward",
    )(grad_out, saved_input, keep_bits, gain.reshape(1, depth))
    grad_in, share = pl.pallas_call(
        store,
        out_shape=(
            jax.ShapeDtypeStruct((rows, depth), jnp.bfloat16),
            jax.ShapeDtypeStruct((1, width), f32),
        ),
        in_specs=[pl.BlockSpec(memory_space=pltpu.VMEM)] * 2,
        out_specs=[pl.BlockSpec(memory_space=pl.ANY)] * 2,
        scratch_shapes=[pltpu.SemaphoreType.DMA((STORES + 1,))],
        name="store_results",
    )(*(pltpu.with_memory_space_constraint(x, pltpu.VMEM) for x in (grad_in, share)))
    return (grad_in, share.reshape(width))


def per_device(grad_out, saved_input, keep_bits, gain):
    fits = grad_out.shape[1] % LANES == 0 and saved_input.shape[0] % CHUNK_ROWS == 0
    fits = fits and keep_bits.shape[1] == LANES
    n_ba = lax.axis_size("ba")
    fits = fits and n_ba > 1 and n_ba & (n_ba - 1) == 0
    body = fused if fits else plain
    return body(grad_out, saved_input, keep_bits, gain)


def solution(mesh):
    placed = (P("aa", "ba"), P(("aa", "ba"), None), P(("aa", "ba"), None), P())
    return jax.shard_map(
        per_device,
        mesh=mesh,
        in_specs=placed,
        out_specs=(P(("aa", "ba"), None), P("ba")),
        check_vma=False,
    )
```

profile of v0, /device:TPU:0, one launch (start us, length us, event | category | flops | bytes accessed | tf_op | source)
XLA Modules:
  0.0 25.1 jit_solution(5713802601842031932)
XLA Ops:
  0.6 23.5 %regroup_backward.1 = (bf16[128,4096]{1,0:T(8,128)(2,1)S(1)}, f32[1,512]{1,0:T(1,128)S(1)}) custom-call(bf16[1024,512]{1,0:T(8,128)(2,1)} %grad_hbm.1, bf16[128,4096]{1,0:T(8,128)(2,1)} %input_hbm.1, s32[128,128]{1,0:T(8,128)} %bits_hbm.1, f32[1,4096]{1,0:T(1,128)} %bitcast.2), custom_call_target="tpu_custom_call" | custom-call | tf_op jit(solution)/shard_map/regroup_backward/pallas_call | solution.py:314
  24.1 1.0 %store_results.1 = (bf16[128,4096]{1,0:T(8,128)(2,1)}, f32[1,512]{1,0:T(1,128)}) custom-call(bf16[128,4096]{1,0:T(8,128)(2,1)S(1)} %get-tuple-element.6.grad_vmem, f32[1,512]{1,0:T(1,128)S(1)} %get-tuple-element.7.share_vmem), custom_call_target="tpu_custom_call" | custom-call | tf_op jit(solution)/shard_map/store_results/pallas_call | solution.py:354
where the time goes:
time: 25.3 us; the launch traced here: 25.1 us
  Pallas kernels  24.5 us (97%)
  between operations  0.64 us (3%)
    pallas_call x1, Pallas kernels, fused(): pl.pallas_call(functools.partial(kernel, n_ba, n_aa), out_shape=(pltpu.VM...  23.5 us
    pallas_call x1, Pallas kernels, fused(): pl.pallas_call(store, out_shape=(jax.ShapeDtypeStruct((rows, depth), jnp....  1.01 us

commit v1 on v0

v1 whole, which is shorter than its diff:
```python
import functools
import math

import jax
import jax.numpy as jnp
from jax import lax
from jax.experimental import pallas as pl
from jax.experimental.pallas import tpu as pltpu
from jax.sharding import PartitionSpec as P

KEEP_RATE = 0.9
EPSILON = 1e-06
LANES = 128
CHUNK_ROWS = 64
STORES = 4
FIRST_ROWS = 32
EARLY_ROWS = 64
MESH = pl.DeviceIdType.MESH


def unpack_bits(words):
    shifts = jnp.arange(32, dtype=jnp.int32)
    bits = jnp.right_shift(words[:, :, None], shifts[None, None, :]) & 1
    return bits.reshape(words.shape[0], words.shape[1] * 32).astype(jnp.float32)


def rows_backward(grad_rows, input_rows, word_rows, gain):
    keep = unpack_bits(word_rows)
    dropped = input_rows.astype(jnp.float32) * keep * (1.0 / KEEP_RATE)
    inverse = lax.rsqrt(jnp.mean(dropped * dropped, axis=-1, keepdims=True) + EPSILON)
    normed = dropped * inverse
    grads = grad_rows.astype(jnp.float32)
    scaled = gain[None, :] * grads
    centre = jnp.mean(scaled * normed, axis=-1, keepdims=True)
    grad_in = (inverse * (scaled - normed * centre) * keep * (1.0 / KEEP_RATE)).astype(jnp.bfloat16)
    partial_sum = jnp.sum(grads * normed, axis=0)
    return (grad_in, partial_sum)


def plain(grad_out, saved_input, keep_bits, gain):
    groups = lax.axis_size("ba")
    rows = grad_out.shape[0] // groups
    pieces = grad_out.reshape(groups, rows, grad_out.shape[1])
    arrived = lax.all_to_all(pieces, "ba", split_axis=0, concat_axis=2, tiled=True)
    grad_rows = arrived.reshape(rows, arrived.shape[2])
    grad_in, partial_sum = rows_backward(grad_rows, saved_input, keep_bits, gain)
    total_tokens = rows * groups * lax.axis_size("aa")
    owned = lax.psum_scatter(partial_sum, "ba", scatter_dimension=0, tiled=True)
    share = lax.psum(owned, "aa")
    gain_grad = share * (1.0 / math.sqrt(total_tokens))
    return (grad_in, gain_grad)


def hops(step):
    return (step >> 1).bit_count()


def steps_with(n_ba, count):
    return sorted((step for step in range(n_ba) if hops(step) == count), key=lambda step: (step % 2, step))


def kernel(n_ba, n_aa, grad_hbm, input_hbm, bits_hbm, gain_hbm, out_ref, share_ref,
           staged, arrived, held, words, gain_ref, normed, masked_gain, outer, totals, sums,
           parts, slices, tails, stage_sem, load_sem, send_sem, small_send, early_recv,
           last_recv, diagonal_recv, sibling_recv, part_recv, tail_recv, ready, flood):
    ba, aa = lax.axis_index("ba"), lax.axis_index("aa")
    rows, width = arrived.shape[1], arrived.shape[2]
    depth = n_ba * width
    chunks = rows // CHUNK_ROWS
    tiles = width // LANES
    direct, diagonal = steps_with(n_ba, 1), steps_with(n_ba, 2)
    n_direct, n_diagonal = len(direct), len(diagonal)
    half = n_direct // 2
    group = n_direct + n_diagonal + 1
    order = [0, 1] + direct + diagonal
    slot = {step: place for place, step in enumerate(order)}
    swap = lax.rem(ba // (2 * direct[0]), 2)
    arrivals = [
        (side + offset, 2 + (half if side else 0) + index)
        for offset, index in ((2 + 2 * swap, swap), (4 - 2 * swap, 1 - swap))
        for side in range(2)
    ]
    early, last = (0, EARLY_ROWS), (EARLY_ROWS, rows - EARLY_ROWS)

    def remote_copy(source, target, send, recv, device):
        return pltpu.make_async_remote_copy(
            src_ref=source, dst_ref=target, send_sem=send, recv_sem=recv,
            device_id=device, device_id_type=MESH,
        )

    def column(step):
        return lax.rem(aa + step, n_aa)

    def rows_of(chunk):
        start = chunk * CHUNK_ROWS
        if not isinstance(start, int):
            start = pl.multiple_of(start, CHUNK_ROWS)
        return pl.ds(start, CHUNK_ROWS)

    def stage(step, semaphore):
        first = pl.ds(pl.multiple_of((ba ^ step) * rows, CHUNK_ROWS), rows)
        target = staged.at[slot[step]] if step else arrived.at[0]
        return pltpu.make_async_copy(grad_hbm.at[first], target, semaphore)

    def piece(step, recv, block=None, place=None):
        place = slot[step] if place is None else place
        at = (place, pl.ds(*block)) if block else (place,)
        return remote_copy(staged.at[at], arrived.at[at], send_sem, recv, {"ba": ba ^ step})

    def early_piece(step):
        return piece(step, early_recv, early)

    def last_piece(step, place):
        return piece(step, last_recv.at[place - 2], last, place)

    def landed(recv, *at):
        return remote_copy(staged.at[at], arrived.at[at], send_sem, recv, {"ba": ba ^ 1})

    def part():
        return remote_copy(parts.at[1], slices.at[1], small_send, part_recv, {"ba": ba ^ 1})

    def share(step):
        mine = tails.at[aa * group]
        return remote_copy(mine, mine, small_send, tail_recv, {"aa": column(step)})

    def late(target, step, place):
        return remote_copy(
            parts.at[place], tails.at[aa * group + place - 1], small_send, tail_recv,
            {"aa": target, "ba": ba ^ step},
        )

    def greet_column(semaphore):
        @pl.when(aa > 0)
        def _():
            pl.semaphore_signal(semaphore, inc=1, device_id={"aa": aa - 1}, device_id_type=MESH)

        @pl.when(aa < n_aa - 1)
        def _():
            pl.semaphore_signal(semaphore, inc=1, device_id={"aa": aa + 1}, device_id_type=MESH)

    column_peers = (aa > 0).astype(jnp.int32) + (aa < n_aa - 1).astype(jnp.int32)

    barrier = pltpu.get_barrier_semaphore()
    for step in direct + [1]:
        pl.semaphore_signal(barrier, inc=1, device_id={"ba": ba ^ step}, device_id_type=MESH)
    greet_column(barrier)
    for step in order[1:]:
        stage(step, stage_sem).start()
    loads = [
        pltpu.make_async_copy(bits_hbm, words, load_sem),
        pltpu.make_async_copy(gain_hbm, gain_ref, load_sem),
        pltpu.make_async_copy(input_hbm, held, load_sem),
        stage(0, load_sem),
    ]
    for load in loads:
        load.start()
    with jax.named_scope("w_barrier"):
        pl.semaphore_wait(barrier, n_direct + 1 + column_peers)
    pl.semaphore_signal(ready, inc=1, device_id={"ba": ba ^ direct[0]}, device_id_type=MESH)
    with jax.named_scope("w_stage"):
        everything = pl.ds(1, n_ba - 1)
        pltpu.make_async_copy(staged.at[everything], staged.at[everything], stage_sem).wait()
    for step in direct:
        early_piece(step).start()
    piece(1, sibling_recv).start()
    with jax.named_scope("w_ready"):
        pl.semaphore_wait(ready, 1)
    greet_column(flood.at[0])
    for step in diagonal:
        piece(step, diagonal_recv).start()
    for step in direct:
        last_piece(step, slot[step]).start()
    with jax.named_scope("w_load"):
        for load in loads:
            load.wait()

    lane = lax.broadcasted_iota(jnp.int32, (CHUNK_ROWS, LANES), 1)
    word_of = lane // 32
    flag = jnp.left_shift(jnp.int32(1), lane % 32)

    def span(source, tile):
        return pl.ds(pl.multiple_of(source * width + tile * LANES, LANES), LANES)

    def prepare(chunk, carry):
        block = rows_of(chunk)

        def drop(source, squares):
            row_words = words[block, :]
            for tile in range(tiles):
                at = span(source, tile)
                index = word_of + (source * tiles + tile) * (LANES // 32)
                spread = jnp.take_along_axis(row_words, index, axis=1, mode="promise_in_bounds")
                kept = (spread & flag) != 0
                dropped = jnp.where(kept, held[block, at].astype(jnp.float32), 0.0) * (1.0 / KEEP_RATE)
                normed[block, at] = dropped
                masked_gain[block, at] = jnp.where(kept, gain_ref[:, at], 0.0)
                squares = squares + dropped * dropped
            return squares

        squares = lax.fori_loop(0, n_ba, drop, jnp.zeros((CHUNK_ROWS, LANES), jnp.float32))
        mean = jnp.sum(squares, axis=1, keepdims=True) * (1.0 / depth)
        inverse = lax.rsqrt(mean + EPSILON)
        outer[block, :] = jnp.broadcast_to(inverse * (1.0 / KEEP_RATE), (CHUNK_ROWS, LANES))

        def scale(source, none):
            for tile in range(tiles):
                at = span(source, tile)
                normed[block, at] = normed[block, at] * inverse
            return none

        lax.fori_loop(0, n_ba, scale, 0)
        return carry

    with jax.named_scope("prepare"):
        lax.fori_loop(0, chunks, prepare, 0)
    sums[...] = jnp.zeros_like(sums)
    totals[...] = jnp.zeros_like(totals)

    def first(step, place, start, size):
        source = ba ^ step

        def some(index, none):
            block = pl.ds(pl.multiple_of(start + index * FIRST_ROWS, FIRST_ROWS), FIRST_ROWS)
            total = totals[block, :]
            for tile in range(tiles):
                at = span(source, tile)
                here = slice(tile * LANES, (tile + 1) * LANES)
                grads = arrived[place, block, here].astype(jnp.float32)
                product = grads * normed[block, at]
                total = total + product * gain_ref[:, at]
                sums[place, :, here] += jnp.sum(product.reshape(FIRST_ROWS // 8, 8, LANES), axis=0)
            totals[block, :] = total
            return none

        lax.fori_loop(0, size // FIRST_ROWS, some, 0)

    def finish(chunk, none):
        block = rows_of(chunk)
        factor = outer[block, :]
        centre = jnp.sum(totals[block, :], axis=1, keepdims=True) * (1.0 / depth)

        for step in order:
            for tile in range(tiles):
                at = span(ba ^ step, tile)
                grads = arrived[slot[step], block, tile * LANES:(tile + 1) * LANES].astype(jnp.float32)
                value = factor * (masked_gain[block, at] * grads - normed[block, at] * centre)
                out_ref[block, at] = value.astype(jnp.bfloat16)
        return none

    def fold(place):
        return jnp.sum(sums[place], axis=0, keepdims=True)

    def send_late(step, place):
        parts[place] = fold(place)
        for target in range(n_aa):
            late(target, step, place).start()

    def meet(turn):
        with jax.named_scope(f"w_flood{turn}"):
            pl.semaphore_wait(flood.at[turn], column_peers)
        if turn < n_aa - 2:
            greet_column(flood.at[turn + 1])

    first(0, 0, 0, rows)
    slices[0] = fold(0)
    with jax.named_scope("w_sibling"):
        piece(1, sibling_recv).wait_recv()
    first(1, 1, 0, rows)
    parts[1] = fold(1)
    part().start()
    meet(0)
    with jax.named_scope("w_early"):
        landed(early_recv, pl.ds(2, n_direct), pl.ds(*early)).wait_recv()
    for step in direct:
        first(step, slot[step], *early)
    for turn in range(1, n_aa - 1):
        meet(turn)
    with jax.named_scope("w_part"):
        part().wait_recv()
    tails[aa * group] = slices[0] + slices[1]
    for step in range(1, n_aa):
        share(step).start()
    with jax.named_scope("w_diag"):
        landed(diagonal_recv, pl.ds(2 + n_direct, n_diagonal)).wait_recv()
    for step in diagonal:
        first(step, slot[step], 0, rows)
        send_late(step, slot[step])
    for step, place in arrivals:
        with jax.named_scope("w_last"):
            last_piece(step, place).wait_recv()
        first(step, place, *last)
        send_late(step, place)
    with jax.named_scope("finish"):
        lax.fori_loop(0, chunks, finish, 0)
    with jax.named_scope("w_tail"):
        others = tails.at[pl.ds(0, n_aa * group - 1)]
        remote_copy(others, others, small_send, tail_recv, {"ba": ba ^ 1}).wait_recv()
    with jax.named_scope("final_sum"):
        total = jnp.sum(tails[...], axis=0)
        share_ref[...] = total * (1.0 / math.sqrt(rows * n_ba * n_aa))
    with jax.named_scope("w_last_sends"):
        landed(sibling_recv, everything).wait_send()
        remote_copy(tails, tails, small_send, tail_recv, {"ba": ba ^ 1}).wait_send()


def store(grad_vmem, share_vmem, grad_hbm, share_hbm, sem):
    rows = grad_vmem.shape[0] // STORES
    copies = [pltpu.make_async_copy(share_vmem, share_hbm, sem.at[1])]
    for index in range(STORES):
        block = pl.ds(index * rows, rows)
        copies.append(pltpu.make_async_copy(grad_vmem.at[block], grad_hbm.at[block], sem.at[0]))
    for copy in copies:
        copy.start()
    pltpu.make_async_copy(grad_vmem, grad_hbm, sem.at[0]).wait()
    copies[0].wait()


def fused(grad_out, saved_input, keep_bits, gain):
    n_ba, n_aa = lax.axis_size("ba"), lax.axis_size("aa")
    width = grad_out.shape[1]
    rows, depth = saved_input.shape
    n_direct, n_diagonal = len(steps_with(n_ba, 1)), len(steps_with(n_ba, 2))
    f32 = jnp.float32
    grad_in, share = pl.pallas_call(
        functools.partial(kernel, n_ba, n_aa),
        out_shape=(
            pltpu.VMEM((rows, depth), jnp.bfloat16),
            pltpu.VMEM((1, width), f32),
        ),
        in_specs=[pl.BlockSpec(memory_space=pl.ANY)] * 4,
        out_specs=(pl.BlockSpec(memory_space=pltpu.VMEM), pl.BlockSpec(memory_space=pltpu.VMEM)),
        scratch_shapes=[
            pltpu.VMEM((n_ba, rows, width), jnp.bfloat16),
            pltpu.VMEM((n_ba, rows, width), jnp.bfloat16),
            pltpu.VMEM((rows, depth), jnp.bfloat16),
            pltpu.VMEM(keep_bits.shape, jnp.int32),
            pltpu.VMEM((1, depth), f32),
            pltpu.VMEM((rows, depth), f32),
            pltpu.VMEM((rows, depth), f32),
            pltpu.VMEM((rows, LANES), f32),
            pltpu.VMEM((rows, LANES), f32),
            pltpu.VMEM((n_ba, 8, width), f32),
            pltpu.VMEM((n_ba, 1, width), f32),
            pltpu.VMEM((2, 1, width), f32),
            pltpu.VMEM((n_aa * (n_direct + n_diagonal + 1), 1, width), f32),
            pltpu.SemaphoreType.DMA,
            pltpu.SemaphoreType.DMA,
            pltpu.SemaphoreType.DMA,
            pltpu.SemaphoreType.DMA,
            pltpu.SemaphoreType.DMA,
            pltpu.SemaphoreType.DMA((n_direct,)),
            pltpu.SemaphoreType.DMA,
            pltpu.SemaphoreType.DMA,
            pltpu.SemaphoreType.DMA,
            pltpu.SemaphoreType.DMA,
            pltpu.SemaphoreType.REGULAR,
            pltpu.SemaphoreType.REGULAR((n_aa - 1,)),
        ],
        compiler_params=pltpu.CompilerParams(collective_id=0, has_side_effects=True),
        name="regroup_backward",
    )(grad_out, saved_input, keep_bits, gain.reshape(1, depth))
    grad_in, share = pl.pallas_call(
        store,
        out_shape=(
            jax.ShapeDtypeStruct((rows, depth), jnp.bfloat16),
            jax.ShapeDtypeStruct((1, width), f32),
        ),
        in_specs=[pl.BlockSpec(memory_space=pltpu.VMEM)] * 2,
        out_specs=[pl.BlockSpec(memory_space=pl.ANY)] * 2,
        scratch_shapes=[pltpu.SemaphoreType.DMA((2,))],
        name="store_results",
    )(*(pltpu.with_memory_space_constraint(x, pltpu.VMEM) for x in (grad_in, share)))
    return (grad_in, share.reshape(width))


def per_device(grad_out, saved_input, keep_bits, gain):
    fits = grad_out.shape[1] % LANES == 0 and saved_input.shape[0] % CHUNK_ROWS == 0
    fits = fits and keep_bits.shape[1] == LANES
    n_ba = lax.axis_size("ba")
    fits = fits and n_ba & (n_ba - 1) == 0 and hops(n_ba - 1) == 2 and lax.axis_size("aa") > 1
    body = fused if fits else plain
    return body(grad_out, saved_input, keep_bits, gain)


def solution(mesh):
    placed = (P("aa", "ba"), P(("aa", "ba"), None), P(("aa", "ba"), None), P())
    return jax.shard_map(
        per_device,
        mesh=mesh,
        in_specs=placed,
        out_specs=(P(("aa", "ba"), None), P("ba")),
        check_vma=False,
    )
```

time: 25.3 us -> 23.4 us (0.925)
  Pallas kernels: 24.5 us -> 22.6 us
    pallas_call x1, Pallas kernels: 23.5 us -> 21.6 us  [fused(): pl.pallas_call(functools.partial(kernel, n_ba, n_aa), out_shape=(pltpu.VM...]
where the time goes in v1:
time: 23.4 us; the launch traced here: 23.2 us
  Pallas kernels  22.6 us (97%)
  between operations  0.64 us (3%)
    pallas_call x1, Pallas kernels, fused(): pl.pallas_call(functools.partial(kernel, n_ba, n_aa), out_shape=(pltpu.VM...  21.6 us
    pallas_call x1, Pallas kernels, fused(): pl.pallas_call(store, out_shape=(jax.ShapeDtypeStruct((rows, depth), jnp....  0.98 us

profile of v1, /device:TPU:0, one launch (start us, length us, event | category | flops | bytes accessed | tf_op | source)
XLA Modules:
  0.0 23.2 jit_solution(3434647508285242060)
XLA Ops:
  0.6 21.6 %regroup_backward.1 = (bf16[128,4096]{1,0:T(8,128)(2,1)S(1)}, f32[1,512]{1,0:T(1,128)S(1)}) custom-call(bf16[1024,512]{1,0:T(8,128)(2,1)} %grad_hbm.1, bf16[128,4096]{1,0:T(8,128)(2,1)} %input_hbm.1, s32[128,128]{1,0:T(8,128)} %bits_hbm.1, f32[1,4096]{1,0:T(1,128)} %bitcast.2), custom_call_target="tpu_custom_call" | custom-call | tf_op jit(solution)/shard_map/regroup_backward/pallas_call | solution.py:324
  22.2 1.0 %store_results.1 = (bf16[128,4096]{1,0:T(8,128)(2,1)}, f32[1,512]{1,0:T(1,128)}) custom-call(bf16[128,4096]{1,0:T(8,128)(2,1)S(1)} %get-tuple-element.6.grad_vmem, f32[1,512]{1,0:T(1,128)S(1)} %get-tuple-element.7.share_vmem), custom_call_target="tpu_custom_call" | custom-call | tf_op jit(solution)/shard_map/store_results/pallas_call | solution.py:362

commit v2 on v1

--- a/solution.py
+++ b/solution.py
@@ -13,8 +13,9 @@
 LANES = 128
 CHUNK_ROWS = 64
 STORES = 4
-FIRST_ROWS = 32
+FIRST_ROWS = 64
 EARLY_ROWS = 64
+CORNER_ROWS = 16
 MESH = pl.DeviceIdType.MESH
 
 
@@ -62,7 +63,8 @@
 def kernel(n_ba, n_aa, grad_hbm, input_hbm, bits_hbm, gain_hbm, out_ref, share_ref,
            staged, arrived, held, words, gain_ref, normed, masked_gain, outer, totals, sums,
            parts, slices, tails, stage_sem, load_sem, send_sem, small_send, early_recv,
-           last_recv, diagonal_recv, sibling_recv, part_recv, tail_recv, ready, flood):
+           last_recv, diagonal_recv, sibling_recv, part_recv, tail_recv, ready, flood,
+           relayed, relay_recv, relay_send, corner_recv):
     ba, aa = lax.axis_index("ba"), lax.axis_index("aa")
     rows, width = arrived.shape[1], arrived.shape[2]
     depth = n_ba * width
@@ -81,6 +83,12 @@
         for side in range(2)
     ]
     early, last = (0, EARLY_ROWS), (EARLY_ROWS, rows - EARLY_ROWS)
+    short, corner = (EARLY_ROWS, rows - EARLY_ROWS - CORNER_ROWS), (rows - CORNER_ROWS, CORNER_ROWS)
+    pairs = n_aa // 2
+    shift = n_aa - pairs
+    side = lax.rem(ba, 2)
+    upper = aa >= shift
+    relays = jnp.logical_and(aa < pairs, side == 1)
 
     def remote_copy(source, target, send, recv, device):
         return pltpu.make_async_remote_copy(
@@ -107,11 +115,28 @@
         at = (place, pl.ds(*block)) if block else (place,)
         return remote_copy(staged.at[at], arrived.at[at], send_sem, recv, {"ba": ba ^ step})
 
-    def early_piece(step):
-        return piece(step, early_recv, early)
-
-    def last_piece(step, place):
-        return piece(step, last_recv.at[place - 2], last, place)
+    def early_piece(step, place):
+        return piece(step, early_recv.at[place - 2], early, place)
+
+    def last_piece(step, place, block):
+        return piece(step, last_recv.at[place - 2], block, place)
+
+    def to_relay(step):
+        target = ba ^ step
+        parity = lax.rem(target, 2)
+        return remote_copy(
+            staged.at[slot[step], pl.ds(*corner)], relayed.at[parity, slot[step] - 2], send_sem, relay_recv,
+            {"aa": aa - shift, "ba": target + 1 - parity},
+        )
+
+    def from_relay(parity, place):
+        return remote_copy(
+            relayed.at[parity, place], arrived.at[place + 2, pl.ds(*corner)], relay_send, corner_recv,
+            {"aa": aa + shift, "ba": ba - 1 + parity},
+        )
+
+    def relay_all():
+        return remote_copy(relayed, relayed, relay_send, relay_recv, {"ba": ba ^ 1})
 
     def landed(recv, *at):
         return remote_copy(staged.at[at], arrived.at[at], send_sem, recv, {"ba": ba ^ 1})
@@ -144,6 +169,13 @@
     for step in direct + [1]:
         pl.semaphore_signal(barrier, inc=1, device_id={"ba": ba ^ step}, device_id_type=MESH)
     greet_column(barrier)
+
+    @pl.when(relays)
+    def _():
+        for step in direct:
+            pl.semaphore_signal(
+                barrier, inc=1, device_id={"aa": aa + shift, "ba": ba ^ step}, device_id_type=MESH)
+
     for step in order[1:]:
         stage(step, stage_sem).start()
     loads = [
@@ -155,21 +187,35 @@
     for load in loads:
         load.start()
     with jax.named_scope("w_barrier"):
-        pl.semaphore_wait(barrier, n_direct + 1 + column_peers)
+        pl.semaphore_wait(barrier, n_direct + 1 + column_peers + half * upper.astype(jnp.int32))
     pl.semaphore_signal(ready, inc=1, device_id={"ba": ba ^ direct[0]}, device_id_type=MESH)
     with jax.named_scope("w_stage"):
         everything = pl.ds(1, n_ba - 1)
         pltpu.make_async_copy(staged.at[everything], staged.at[everything], stage_sem).wait()
     for step in direct:
-        early_piece(step).start()
+        early_piece(step, slot[step]).start()
+    @pl.when(upper)
+    def _():
+        for step in direct:
+            to_relay(step).start()
+
     piece(1, sibling_recv).start()
     with jax.named_scope("w_ready"):
         pl.semaphore_wait(ready, 1)
     greet_column(flood.at[0])
     for step in diagonal:
         piece(step, diagonal_recv).start()
-    for step in direct:
-        last_piece(step, slot[step]).start()
+
+    @pl.when(upper)
+    def _():
+        for step in direct:
+            last_piece(step, slot[step], short).start()
+
+    @pl.when(jnp.logical_not(upper))
+    def _():
+        for step in direct:
+            last_piece(step, slot[step], last).start()
+
     with jax.named_scope("w_load"):
         for load in loads:
             load.wait()
@@ -217,10 +263,10 @@
     totals[...] = jnp.zeros_like(totals)
 
     def first(step, place, start, size):
-        source = ba ^ step
+        source, count = ba ^ step, math.gcd(start, size, FIRST_ROWS)
 
         def some(index, none):
-            block = pl.ds(pl.multiple_of(start + index * FIRST_ROWS, FIRST_ROWS), FIRST_ROWS)
+            block = pl.ds(pl.multiple_of(start + index * count, count), count)
             total = totals[block, :]
             for tile in range(tiles):
                 at = span(source, tile)
@@ -228,11 +274,11 @@
                 grads = arrived[place, block, here].astype(jnp.float32)
                 product = grads * normed[block, at]
                 total = total + product * gain_ref[:, at]
-                sums[place, :, here] += jnp.sum(product.reshape(FIRST_ROWS // 8, 8, LANES), axis=0)
+                sums[place, :, here] += jnp.sum(product.reshape(count // 8, 8, LANES), axis=0)
             totals[block, :] = total
             return none
 
-        lax.fori_loop(0, size // FIRST_ROWS, some, 0)
+        lax.fori_loop(0, size // count, some, 0)
 
     def finish(chunk, none):
         block = rows_of(chunk)
@@ -260,6 +306,12 @@
             pl.semaphore_wait(flood.at[turn], column_peers)
         if turn < n_aa - 2:
             greet_column(flood.at[turn + 1])
+
+    def take_early(steps):
+        for step, place in steps:
+            with jax.named_scope("w_early"):
+                early_piece(step, place).wait_recv()
+            first(step, place, *early)
 
     first(0, 0, 0, rows)
     slices[0] = fold(0)
@@ -269,10 +321,15 @@
     parts[1] = fold(1)
     part().start()
     meet(0)
-    with jax.named_scope("w_early"):
-        landed(early_recv, pl.ds(2, n_direct), pl.ds(*early)).wait_recv()
-    for step in direct:
-        first(step, slot[step], *early)
+
+    @pl.when(relays)
+    def _():
+        with jax.named_scope("w_relay"):
+            relay_all().wait_recv()
+        for parity in range(2):
+            for place in range(n_direct):
+                from_relay(parity, place).start()
+
     for turn in range(1, n_aa - 1):
         meet(turn)
     with jax.named_scope("w_part"):
@@ -280,16 +337,37 @@
     tails[aa * group] = slices[0] + slices[1]
     for step in range(1, n_aa):
         share(step).start()
+    take_early(arrivals[:half])
     with jax.named_scope("w_diag"):
         landed(diagonal_recv, pl.ds(2 + n_direct, n_diagonal)).wait_recv()
     for step in diagonal:
         first(step, slot[step], 0, rows)
         send_late(step, slot[step])
-    for step, place in arrivals:
-        with jax.named_scope("w_last"):
-            last_piece(step, place).wait_recv()
-        first(step, place, *last)
-        send_late(step, place)
+
+    @pl.when(upper)
+    def _():
+        with jax.named_scope("w_corner"):
+            landed(corner_recv, pl.ds(2, n_direct), pl.ds(*corner)).wait_recv()
+        for step in direct:
+            first(step, slot[step], *corner)
+
+    for stage_index, some_arrivals in enumerate((arrivals[:half], arrivals[half:])):
+        if stage_index:
+            take_early(some_arrivals)
+        for step, place in some_arrivals:
+            @pl.when(upper)
+            def _(step=step, place=place):
+                with jax.named_scope("w_last"):
+                    last_piece(step, place, short).wait_recv()
+                first(step, place, *short)
+
+            @pl.when(jnp.logical_not(upper))
+            def _(step=step, place=place):
+                with jax.named_scope("w_last"):
+                    last_piece(step, place, last).wait_recv()
+                first(step, place, *last)
+
+            send_late(step, place)
     with jax.named_scope("finish"):
         lax.fori_loop(0, chunks, finish, 0)
     with jax.named_scope("w_tail"):
@@ -300,6 +378,11 @@
         share_ref[...] = total * (1.0 / math.sqrt(rows * n_ba * n_aa))
     with jax.named_scope("w_last_sends"):
         landed(sibling_recv, everything).wait_send()
+
+        @pl.when(relays)
+        def _():
+            relay_all().wait_send()
+
         remote_copy(tails, tails, small_send, tail_recv, {"ba": ba ^ 1}).wait_send()
 
 
@@ -347,7 +430,7 @@
             pltpu.SemaphoreType.DMA,
             pltpu.SemaphoreType.DMA,
             pltpu.SemaphoreType.DMA,
-            pltpu.SemaphoreType.DMA,
+            pltpu.SemaphoreType.DMA((n_direct,)),
             pltpu.SemaphoreType.DMA((n_direct,)),
             pltpu.SemaphoreType.DMA,
             pltpu.SemaphoreType.DMA,
@@ -355,6 +438,10 @@
             pltpu.SemaphoreType.DMA,
             pltpu.SemaphoreType.REGULAR,
             pltpu.SemaphoreType.REGULAR((n_aa - 1,)),
+            pltpu.VMEM((2, n_direct, CORNER_ROWS, width), jnp.bfloat16),
+            pltpu.SemaphoreType.DMA,
+            pltpu.SemaphoreType.DMA,
+            pltpu.SemaphoreType.DMA,
         ],
         compiler_params=pltpu.CompilerParams(collective_id=0, has_side_effects=True),
         name="regroup_backward",

time: 23.4 us -> 22.8 us (0.974)
  Pallas kernels: 22.6 us -> 22 us
    pallas_call x1, Pallas kernels: 21.6 us -> 21 us  [fused(): pl.pallas_call(functools.partial(kernel, n_ba, n_aa), out_shape=(pltpu.VM...]
where the time goes in v2:
time: 22.8 us; the launch traced here: 22.6 us
  Pallas kernels  22 us (96%)
  between operations  0.64 us (3%)
    pallas_call x1, Pallas kernels, fused(): pl.pallas_call(functools.partial(kernel, n_ba, n_aa), out_shape=(pltpu.VM...  21 us
    pallas_call x1, Pallas kernels, fused(): pl.pallas_call(store, out_shape=(jax.ShapeDtypeStruct((rows, depth), jnp....  0.98 us

profile of v2, /device:TPU:0, one launch (start us, length us, event | category | flops | bytes accessed | tf_op | source)
XLA Modules:
  0.0 22.6 jit_solution(15310531871620588577)
XLA Ops:
  0.6 21.0 %regroup_backward.1 = (bf16[128,4096]{1,0:T(8,128)(2,1)S(1)}, f32[1,512]{1,0:T(1,128)S(1)}) custom-call(bf16[1024,512]{1,0:T(8,128)(2,1)} %grad_hbm.1, bf16[128,4096]{1,0:T(8,128)(2,1)} %input_hbm.1, s32[128,128]{1,0:T(8,128)} %bits_hbm.1, f32[1,4096]{1,0:T(1,128)} %bitcast.2), custom_call_target="tpu_custom_call" | custom-call | tf_op jit(solution)/shard_map/regroup_backward/pallas_call | solution.py:407
  21.6 1.0 %store_results.1 = (bf16[128,4096]{1,0:T(8,128)(2,1)}, f32[1,512]{1,0:T(1,128)}) custom-call(bf16[128,4096]{1,0:T(8,128)(2,1)S(1)} %get-tuple-element.6.grad_vmem, f32[1,512]{1,0:T(1,128)S(1)} %get-tuple-element.7.share_vmem), custom_call_target="tpu_custom_call" | custom-call | tf_op jit(solution)/shard_map/store_results/pallas_call | solution.py:449

commit v3 on v1

--- a/solution.py
+++ b/solution.py
@@ -13,8 +13,9 @@
 LANES = 128
 CHUNK_ROWS = 64
 STORES = 4
-FIRST_ROWS = 32
+FIRST_ROWS = 64
 EARLY_ROWS = 64
+RELAY_ROWS = 16
 MESH = pl.DeviceIdType.MESH
 
 
@@ -62,7 +63,8 @@
 def kernel(n_ba, n_aa, grad_hbm, input_hbm, bits_hbm, gain_hbm, out_ref, share_ref,
            staged, arrived, held, words, gain_ref, normed, masked_gain, outer, totals, sums,
            parts, slices, tails, stage_sem, load_sem, send_sem, small_send, early_recv,
-           last_recv, diagonal_recv, sibling_recv, part_recv, tail_recv, ready, flood):
+           last_recv, diagonal_recv, sibling_recv, part_recv, tail_recv, ready, flood,
+           relayed, relay_recv, relay_send, corner_recv):
     ba, aa = lax.axis_index("ba"), lax.axis_index("aa")
     rows, width = arrived.shape[1], arrived.shape[2]
     depth = n_ba * width
@@ -71,7 +73,7 @@
     direct, diagonal = steps_with(n_ba, 1), steps_with(n_ba, 2)
     n_direct, n_diagonal = len(direct), len(diagonal)
     half = n_direct // 2
-    group = n_direct + n_diagonal + 1
+    per_plane = n_direct + n_diagonal + 1
     order = [0, 1] + direct + diagonal
     slot = {step: place for place, step in enumerate(order)}
     swap = lax.rem(ba // (2 * direct[0]), 2)
@@ -80,7 +82,41 @@
         for offset, index in ((2 + 2 * swap, swap), (4 - 2 * swap, 1 - swap))
         for side in range(2)
     ]
-    early, last = (0, EARLY_ROWS), (EARLY_ROWS, rows - EARLY_ROWS)
+    groups = (arrivals[:half], arrivals[half:])
+    early = (0, EARLY_ROWS)
+    first_chip = ba < 2
+    beside = (ba ^ groups[0][0][0]) < 2
+    never = ba < 0
+
+    def amounts(plane, near_first):
+        top = plane == n_aa - 1
+        second = plane == n_aa - 2 if n_aa > 3 else never
+        both = jnp.logical_and
+        one = jnp.logical_or(both(top, jnp.logical_not(near_first)), both(second, near_first))
+        return {1: one, 2: both(top, near_first)}
+
+    mirror = n_aa - 1 - aa
+    odd = lax.rem(ba, 2) == 1
+    sends = amounts(aa, first_chip)
+    fed = (amounts(aa, beside), amounts(aa, never))
+    relays = tuple(
+        {count: jnp.logical_and(flag, odd) for count, flag in amounts(mirror, near).items()}
+        for near in (beside, never)
+    )
+
+    def either(flags):
+        return jnp.logical_or(flags[1], flags[2])
+
+    def last(count):
+        return (EARLY_ROWS, rows - EARLY_ROWS - count * RELAY_ROWS)
+
+    def relay_block(index, count=1):
+        return pl.ds(rows - (index + count) * RELAY_ROWS, count * RELAY_ROWS)
+
+    def for_count(flags, action):
+        for count, flag in flags.items():
+            pl.when(flag)(functools.partial(action, count))
+        pl.when(jnp.logical_not(either(flags)))(functools.partial(action, 0))
 
     def remote_copy(source, target, send, recv, device):
         return pltpu.make_async_remote_copy(
@@ -107,11 +143,31 @@
         at = (place, pl.ds(*block)) if block else (place,)
         return remote_copy(staged.at[at], arrived.at[at], send_sem, recv, {"ba": ba ^ step})
 
-    def early_piece(step):
-        return piece(step, early_recv, early)
-
-    def last_piece(step, place):
-        return piece(step, last_recv.at[place - 2], last, place)
+    def early_piece(step, place):
+        return piece(step, early_recv.at[place - 2], early, place)
+
+    def last_piece(step, place, block):
+        return piece(step, last_recv.at[place - 2], block, place)
+
+    def to_relay(step, index):
+        target = ba ^ step
+        parity = lax.rem(target, 2)
+        swapped = lax.rem(target // (2 * direct[0]), 2)
+        group = 1 - swapped if step >= 2 * direct[0] else swapped
+        return remote_copy(
+            staged.at[slot[step], relay_block(index)], relayed.at[group, index, parity, step % 2],
+            send_sem, relay_recv.at[group], {"aa": mirror, "ba": target + 1 - parity},
+        )
+
+    def from_relay(group, index, parity, cross):
+        return remote_copy(
+            relayed.at[group, index, parity, cross], arrived.at[groups[group][cross][1], relay_block(index)],
+            relay_send.at[group], corner_recv.at[group], {"aa": mirror, "ba": ba - 1 + parity},
+        )
+
+    def relay_all(group, count):
+        blocks = relayed.at[group, pl.ds(0, count)]
+        return remote_copy(blocks, blocks, relay_send.at[group], relay_recv.at[group], {"ba": ba ^ 1})
 
     def landed(recv, *at):
         return remote_copy(staged.at[at], arrived.at[at], send_sem, recv, {"ba": ba ^ 1})
@@ -120,12 +176,12 @@
         return remote_copy(parts.at[1], slices.at[1], small_send, part_recv, {"ba": ba ^ 1})
 
     def share(step):
-        mine = tails.at[aa * group]
+        mine = tails.at[aa * per_plane]
         return remote_copy(mine, mine, small_send, tail_recv, {"aa": column(step)})
 
     def late(target, step, place):
         return remote_copy(
-            parts.at[place], tails.at[aa * group + place - 1], small_send, tail_recv,
+            parts.at[place], tails.at[aa * per_plane + place - 1], small_send, tail_recv,
             {"aa": target, "ba": ba ^ step},
         )
 
@@ -144,6 +200,14 @@
     for step in direct + [1]:
         pl.semaphore_signal(barrier, inc=1, device_id={"ba": ba ^ step}, device_id_type=MESH)
     greet_column(barrier)
+
+    for group in range(2):
+        @pl.when(either(relays[group]))
+        def _(group=group):
+            for step, _ in groups[group]:
+                pl.semaphore_signal(
+                    barrier, inc=1, device_id={"aa": mirror, "ba": ba ^ step}, device_id_type=MESH)
+
     for step in order[1:]:
         stage(step, stage_sem).start()
     loads = [
@@ -155,21 +219,36 @@
     for load in loads:
         load.start()
     with jax.named_scope("w_barrier"):
-        pl.semaphore_wait(barrier, n_direct + 1 + column_peers)
+        pl.semaphore_wait(barrier, n_direct + 1 + column_peers + half * either(sends).astype(jnp.int32))
     pl.semaphore_signal(ready, inc=1, device_id={"ba": ba ^ direct[0]}, device_id_type=MESH)
     with jax.named_scope("w_stage"):
         everything = pl.ds(1, n_ba - 1)
         pltpu.make_async_copy(staged.at[everything], staged.at[everything], stage_sem).wait()
     for step in direct:
-        early_piece(step).start()
+        early_piece(step, slot[step]).start()
+
+    @pl.when(either(sends))
+    def _():
+        for step in direct:
+            to_relay(step, 0).start()
+
+    @pl.when(sends[2])
+    def _():
+        for step in direct:
+            to_relay(step, 1).start()
+
     piece(1, sibling_recv).start()
     with jax.named_scope("w_ready"):
         pl.semaphore_wait(ready, 1)
     greet_column(flood.at[0])
     for step in diagonal:
         piece(step, diagonal_recv).start()
-    for step in direct:
-        last_piece(step, slot[step]).start()
+
+    def start_last(count):
+        for step in direct:
+            last_piece(step, slot[step], last(count)).start()
+
+    for_count(sends, start_last)
     with jax.named_scope("w_load"):
         for load in loads:
             load.wait()
@@ -217,10 +296,10 @@
     totals[...] = jnp.zeros_like(totals)
 
     def first(step, place, start, size):
-        source = ba ^ step
+        source, count = ba ^ step, math.gcd(start, size, FIRST_ROWS)
 
         def some(index, none):
-            block = pl.ds(pl.multiple_of(start + index * FIRST_ROWS, FIRST_ROWS), FIRST_ROWS)
+            block = pl.ds(pl.multiple_of(start + index * count, count), count)
             total = totals[block, :]
             for tile in range(tiles):
                 at = span(source, tile)
@@ -228,11 +307,11 @@
                 grads = arrived[place, block, here].astype(jnp.float32)
                 product = grads * normed[block, at]
                 total = total + product * gain_ref[:, at]
-                sums[place, :, here] += jnp.sum(product.reshape(FIRST_ROWS // 8, 8, LANES), axis=0)
+                sums[place, :, here] += jnp.sum(product.reshape(count // 8, 8, LANES), axis=0)
             totals[block, :] = total
             return none
 
-        lax.fori_loop(0, size // FIRST_ROWS, some, 0)
+        lax.fori_loop(0, size // count, some, 0)
 
     def finish(chunk, none):
         block = rows_of(chunk)
@@ -260,6 +339,12 @@
             pl.semaphore_wait(flood.at[turn], column_peers)
         if turn < n_aa - 2:
             greet_column(flood.at[turn + 1])
+
+    def take_early(steps):
+        for step, place in steps:
+            with jax.named_scope("w_early"):
+                early_piece(step, place).wait_recv()
+            first(step, place, *early)
 
     first(0, 0, 0, rows)
     slices[0] = fold(0)
@@ -269,37 +354,67 @@
     parts[1] = fold(1)
     part().start()
     meet(0)
-    with jax.named_scope("w_early"):
-        landed(early_recv, pl.ds(2, n_direct), pl.ds(*early)).wait_recv()
-    for step in direct:
-        first(step, slot[step], *early)
+
+    def pass_on(group, count):
+        if count:
+            with jax.named_scope("w_relay"):
+                relay_all(group, count).wait_recv()
+            for index in range(count):
+                for parity in range(2):
+                    for cross in range(2):
+                        from_relay(group, index, parity, cross).start()
+
+    for group in range(2):
+        for_count(relays[group], functools.partial(pass_on, group))
     for turn in range(1, n_aa - 1):
         meet(turn)
     with jax.named_scope("w_part"):
         part().wait_recv()
-    tails[aa * group] = slices[0] + slices[1]
+    tails[aa * per_plane] = slices[0] + slices[1]
     for step in range(1, n_aa):
         share(step).start()
-    with jax.named_scope("w_diag"):
-        landed(diagonal_recv, pl.ds(2 + n_direct, n_diagonal)).wait_recv()
-    for step in diagonal:
-        first(step, slot[step], 0, rows)
-        send_late(step, slot[step])
-    for step, place in arrivals:
-        with jax.named_scope("w_last"):
-            last_piece(step, place).wait_recv()
-        first(step, place, *last)
-        send_late(step, place)
+    def take_diagonal():
+        with jax.named_scope("w_diag"):
+            landed(diagonal_recv, pl.ds(2 + n_direct, n_diagonal)).wait_recv()
+        for step in diagonal:
+            first(step, slot[step], 0, rows)
+            send_late(step, slot[step])
+
+    def take_group(group, count):
+        if count:
+            with jax.named_scope("w_corner"):
+                landed(corner_recv.at[group], pl.ds(2, half), relay_block(0, count)).wait_recv()
+            for step, place in groups[group]:
+                first(step, place, rows - count * RELAY_ROWS, count * RELAY_ROWS)
+        for step, place in groups[group]:
+            with jax.named_scope("w_last"):
+                last_piece(step, place, last(count)).wait_recv()
+            first(step, place, *last(count))
+            send_late(step, place)
+
+    take_early(groups[0])
+    pl.when(jnp.logical_not(beside))(take_diagonal)
+    for_count(fed[0], functools.partial(take_group, 0))
+    pl.when(beside)(take_diagonal)
+    take_early(groups[1])
+    for_count(fed[1], functools.partial(take_group, 1))
     with jax.named_scope("finish"):
         lax.fori_loop(0, chunks, finish, 0)
     with jax.named_scope("w_tail"):
-        others = tails.at[pl.ds(0, n_aa * group - 1)]
+        others = tails.at[pl.ds(0, n_aa * per_plane - 1)]
         remote_copy(others, others, small_send, tail_recv, {"ba": ba ^ 1}).wait_recv()
     with jax.named_scope("final_sum"):
         total = jnp.sum(tails[...], axis=0)
         share_ref[...] = total * (1.0 / math.sqrt(rows * n_ba * n_aa))
     with jax.named_scope("w_last_sends"):
         landed(sibling_recv, everything).wait_send()
+
+        def wait_relay(group, count):
+            if count:
+                relay_all(group, count).wait_send()
+
+        for group in range(2):
+            for_count(relays[group], functools.partial(wait_relay, group))
         remote_copy(tails, tails, small_send, tail_recv, {"ba": ba ^ 1}).wait_send()
 
 
@@ -347,7 +462,7 @@
             pltpu.SemaphoreType.DMA,
             pltpu.SemaphoreType.DMA,
             pltpu.SemaphoreType.DMA,
-            pltpu.SemaphoreType.DMA,
+            pltpu.SemaphoreType.DMA((n_direct,)),
             pltpu.SemaphoreType.DMA((n_direct,)),
             pltpu.SemaphoreType.DMA,
             pltpu.SemaphoreType.DMA,
@@ -355,6 +470,10 @@
             pltpu.SemaphoreType.DMA,
             pltpu.SemaphoreType.REGULAR,
             pltpu.SemaphoreType.REGULAR((n_aa - 1,)),
+            pltpu.VMEM((2, 2, 2, 2, RELAY_ROWS, width), jnp.bfloat16),
+            pltpu.SemaphoreType.DMA((2,)),
+            pltpu.SemaphoreType.DMA((2,)),
+            pltpu.SemaphoreType.DMA((2,)),
         ],
         compiler_params=pltpu.CompilerParams(collective_id=0, has_side_effects=True),
         name="regroup_backward",

time: 23.4 us -> 22.3 us (0.953)
  Pallas kernels: 22.6 us -> 21.5 us
    pallas_call x1, Pallas kernels: 21.6 us -> 20.6 us  [fused(): pl.pallas_call(functools.partial(kernel, n_ba, n_aa), out_shape=(pltpu.VM...]
where the time goes in v3:
time: 22.3 us; the launch traced here: 22.2 us
  Pallas kernels  21.5 us (96%)
  between operations  0.64 us (3%)
    pallas_call x1, Pallas kernels, fused(): pl.pallas_call(functools.partial(kernel, n_ba, n_aa), out_shape=(pltpu.VM...  20.6 us
    pallas_call x1, Pallas kernels, fused(): pl.pallas_call(store, out_shape=(jax.ShapeDtypeStruct((rows, depth), jnp....  0.98 us

profile of v3, /device:TPU:0, one launch (start us, length us, event | category | flops | bytes accessed | tf_op | source)
XLA Modules:
  0.0 22.2 jit_solution(16481777156311967445)
XLA Ops:
  0.6 20.6 %regroup_backward.1 = (bf16[128,4096]{1,0:T(8,128)(2,1)S(1)}, f32[1,512]{1,0:T(1,128)S(1)}) custom-call(bf16[1024,512]{1,0:T(8,128)(2,1)} %grad_hbm.1, bf16[128,4096]{1,0:T(8,128)(2,1)} %input_hbm.1, s32[128,128]{1,0:T(8,128)} %bits_hbm.1, f32[1,4096]{1,0:T(1,128)} %bitcast.2), custom_call_target="tpu_custom_call" | custom-call | tf_op jit(solution)/shard_map/regroup_backward/pallas_call | solution.py:439
  21.2 1.0 %store_results.1 = (bf16[128,4096]{1,0:T(8,128)(2,1)}, f32[1,512]{1,0:T(1,128)}) custom-call(bf16[128,4096]{1,0:T(8,128)(2,1)S(1)} %get-tuple-element.6.grad_vmem, f32[1,512]{1,0:T(1,128)S(1)} %get-tuple-element.7.share_vmem), custom_call_target="tpu_custom_call" | custom-call | tf_op jit(solution)/shard_map/store_results/pallas_call | solution.py:481

commit v4 on v3

--- a/solution.py
+++ b/solution.py
@@ -14,7 +14,7 @@
 CHUNK_ROWS = 64
 STORES = 4
 FIRST_ROWS = 64
-EARLY_ROWS = 64
+EARLY_ROWS = 48
 RELAY_ROWS = 16
 MESH = pl.DeviceIdType.MESH
 
@@ -143,17 +143,20 @@
         at = (place, pl.ds(*block)) if block else (place,)
         return remote_copy(staged.at[at], arrived.at[at], send_sem, recv, {"ba": ba ^ step})
 
-    def early_piece(step, place):
-        return piece(step, early_recv.at[place - 2], early, place)
-
-    def last_piece(step, place, block):
-        return piece(step, last_recv.at[place - 2], block, place)
+    def axis_of(step):
+        return 1 if step >= 2 * direct[0] else 0
+
+    def early_piece(step):
+        return piece(step, early_recv.at[axis_of(step)], early)
+
+    def last_piece(step, block):
+        return piece(step, last_recv.at[axis_of(step)], block)
 
     def to_relay(step, index):
         target = ba ^ step
         parity = lax.rem(target, 2)
         swapped = lax.rem(target // (2 * direct[0]), 2)
-        group = 1 - swapped if step >= 2 * direct[0] else swapped
+        group = 1 - swapped if axis_of(step) else swapped
         return remote_copy(
             staged.at[slot[step], relay_block(index)], relayed.at[group, index, parity, step % 2],
             send_sem, relay_recv.at[group], {"aa": mirror, "ba": target + 1 - parity},
@@ -225,7 +228,7 @@
         everything = pl.ds(1, n_ba - 1)
         pltpu.make_async_copy(staged.at[everything], staged.at[everything], stage_sem).wait()
     for step in direct:
-        early_piece(step, slot[step]).start()
+        early_piece(step).start()
 
     @pl.when(either(sends))
     def _():
@@ -246,7 +249,7 @@
 
     def start_last(count):
         for step in direct:
-            last_piece(step, slot[step], last(count)).start()
+            last_piece(step, last(count)).start()
 
     for_count(sends, start_last)
     with jax.named_scope("w_load"):
@@ -340,10 +343,12 @@
         if turn < n_aa - 2:
             greet_column(flood.at[turn + 1])
 
-    def take_early(steps):
-        for step, place in steps:
-            with jax.named_scope("w_early"):
-                early_piece(step, place).wait_recv()
+    axes = (swap, 1 - swap)
+
+    def take_early(group):
+        with jax.named_scope("w_early"):
+            landed(early_recv.at[axes[group]], pl.ds(2, half), pl.ds(*early)).wait_recv()
+        for step, place in groups[group]:
             first(step, place, *early)
 
     first(0, 0, 0, rows)
@@ -386,17 +391,18 @@
                 landed(corner_recv.at[group], pl.ds(2, half), relay_block(0, count)).wait_recv()
             for step, place in groups[group]:
                 first(step, place, rows - count * RELAY_ROWS, count * RELAY_ROWS)
-        for step, place in groups[group]:
-            with jax.named_scope("w_last"):
-                last_piece(step, place, last(count)).wait_recv()
+        with jax.named_scope("w_last"):
+            landed(last_recv.at[axes[group]], pl.ds(2, half), pl.ds(*last(count))).wait_recv()
+        for cross in (0, 1):
+            step, place = groups[group][cross]
             first(step, place, *last(count))
             send_late(step, place)
 
-    take_early(groups[0])
     pl.when(jnp.logical_not(beside))(take_diagonal)
+    take_early(0)
     for_count(fed[0], functools.partial(take_group, 0))
     pl.when(beside)(take_diagonal)
-    take_early(groups[1])
+    take_early(1)
     for_count(fed[1], functools.partial(take_group, 1))
     with jax.named_scope("finish"):
         lax.fori_loop(0, chunks, finish, 0)
@@ -462,8 +468,8 @@
             pltpu.SemaphoreType.DMA,
             pltpu.SemaphoreType.DMA,
             pltpu.SemaphoreType.DMA,
-            pltpu.SemaphoreType.DMA((n_direct,)),
-            pltpu.SemaphoreType.DMA((n_direct,)),
+            pltpu.SemaphoreType.DMA((2,)),
+            pltpu.SemaphoreType.DMA((2,)),
             pltpu.SemaphoreType.DMA,
             pltpu.SemaphoreType.DMA,
             pltpu.SemaphoreType.DMA,

time: 22.3 us -> 22.1 us (level)
  no operation moved by 1% of the time
where the time goes in v4:
time: 22.1 us; the launch traced here: 22 us
  Pallas kernels  21.3 us (96%)
  between operations  0.64 us (3%)
    pallas_call x1, Pallas kernels, fused(): pl.pallas_call(functools.partial(kernel, n_ba, n_aa), out_shape=(pltpu.VM...  20.4 us
    pallas_call x1, Pallas kernels, fused(): pl.pallas_call(store, out_shape=(jax.ShapeDtypeStruct((rows, depth), jnp....  0.98 us

profile of v4, /device:TPU:0, one launch (start us, length us, event | category | flops | bytes accessed | tf_op | source)
XLA Modules:
  0.0 22.0 jit_solution(651155234063252987)
XLA Ops:
  0.6 20.4 %regroup_backward.1 = (bf16[128,4096]{1,0:T(8,128)(2,1)S(1)}, f32[1,512]{1,0:T(1,128)S(1)}) custom-call(bf16[1024,512]{1,0:T(8,128)(2,1)} %grad_hbm.1, bf16[128,4096]{1,0:T(8,128)(2,1)} %input_hbm.1, s32[128,128]{1,0:T(8,128)} %bits_hbm.1, f32[1,4096]{1,0:T(1,128)} %bitcast.2), custom_call_target="tpu_custom_call" | custom-call | tf_op jit(solution)/shard_map/regroup_backward/pallas_call | solution.py:445
  21.0 1.0 %store_results.1 = (bf16[128,4096]{1,0:T(8,128)(2,1)}, f32[1,512]{1,0:T(1,128)}) custom-call(bf16[128,4096]{1,0:T(8,128)(2,1)S(1)} %get-tuple-element.6.grad_vmem, f32[1,512]{1,0:T(1,128)S(1)} %get-tuple-element.7.share_vmem), custom_call_target="tpu_custom_call" | custom-call | tf_op jit(solution)/shard_map/store_results/pallas_call | solution.py:487

commit v5 on v4

--- a/solution.py
+++ b/solution.py
@@ -16,6 +16,7 @@
 FIRST_ROWS = 64
 EARLY_ROWS = 48
 RELAY_ROWS = 16
+RELAYED = ((2, 2), (1, 1), (1, 1))
 MESH = pl.DeviceIdType.MESH
 
 
@@ -88,24 +89,22 @@
     beside = (ba ^ groups[0][0][0]) < 2
     never = ba < 0
 
-    def amounts(plane, near_first):
+    def kinds(plane, near_first):
         top = plane == n_aa - 1
         second = plane == n_aa - 2 if n_aa > 3 else never
         both = jnp.logical_and
-        one = jnp.logical_or(both(top, jnp.logical_not(near_first)), both(second, near_first))
-        return {1: one, 2: both(top, near_first)}
+        return (both(top, near_first), both(second, near_first), both(top, jnp.logical_not(near_first)))
 
     mirror = n_aa - 1 - aa
     odd = lax.rem(ba, 2) == 1
-    sends = amounts(aa, first_chip)
-    fed = (amounts(aa, beside), amounts(aa, never))
+    sends = kinds(aa, first_chip)
+    fed = (kinds(aa, beside), kinds(aa, never))
     relays = tuple(
-        {count: jnp.logical_and(flag, odd) for count, flag in amounts(mirror, near).items()}
-        for near in (beside, never)
+        tuple(jnp.logical_and(flag, odd) for flag in kinds(mirror, near)) for near in (beside, never)
     )
 
     def either(flags):
-        return jnp.logical_or(flags[1], flags[2])
+        return jnp.logical_or(jnp.logical_or(flags[0], flags[1]), flags[2])
 
     def last(count):
         return (EARLY_ROWS, rows - EARLY_ROWS - count * RELAY_ROWS)
@@ -113,10 +112,17 @@
     def relay_block(index, count=1):
         return pl.ds(rows - (index + count) * RELAY_ROWS, count * RELAY_ROWS)
 
-    def for_count(flags, action):
-        for count, flag in flags.items():
-            pl.when(flag)(functools.partial(action, count))
-        pl.when(jnp.logical_not(either(flags)))(functools.partial(action, 0))
+    def for_kind(flags, action):
+        for blocks, flag in zip(RELAYED, flags):
+            pl.when(flag)(functools.partial(action, blocks))
+        pl.when(jnp.logical_not(either(flags)))(functools.partial(action, (0, 0)))
+
+    def for_core(blocks, action):
+        if blocks[0] == blocks[1]:
+            action(blocks[0])
+        else:
+            pl.when(odd)(functools.partial(action, blocks[1]))
+            pl.when(jnp.logical_not(odd))(functools.partial(action, blocks[0]))
 
     def remote_copy(source, target, send, recv, device):
         return pltpu.make_async_remote_copy(
@@ -230,15 +236,15 @@
     for step in direct:
         early_piece(step).start()
 
-    @pl.when(either(sends))
-    def _():
-        for step in direct:
-            to_relay(step, 0).start()
-
-    @pl.when(sends[2])
-    def _():
-        for step in direct:
-            to_relay(step, 1).start()
+    def start_relays(blocks):
+        def start(count):
+            for index in range(count):
+                for step in direct:
+                    to_relay(step, index).start()
+
+        for_core(blocks, start)
+
+    for_kind(sends, start_relays)
 
     piece(1, sibling_recv).start()
     with jax.named_scope("w_ready"):
@@ -247,11 +253,14 @@
     for step in diagonal:
         piece(step, diagonal_recv).start()
 
-    def start_last(count):
-        for step in direct:
-            last_piece(step, last(count)).start()
-
-    for_count(sends, start_last)
+    def start_last(blocks):
+        def start(count):
+            for step in direct:
+                last_piece(step, last(count)).start()
+
+        for_core(blocks, start)
+
+    for_kind(sends, start_last)
     with jax.named_scope("w_load"):
         for load in loads:
             load.wait()
@@ -299,10 +308,9 @@
     totals[...] = jnp.zeros_like(totals)
 
     def first(step, place, start, size):
-        source, count = ba ^ step, math.gcd(start, size, FIRST_ROWS)
-
-        def some(index, none):
-            block = pl.ds(pl.multiple_of(start + index * count, count), count)
+        source = ba ^ step
+
+        def some(block, count):
             total = totals[block, :]
             for tile in range(tiles):
                 at = span(source, tile)
@@ -312,9 +320,15 @@
                 total = total + product * gain_ref[:, at]
                 sums[place, :, here] += jnp.sum(product.reshape(count // 8, 8, LANES), axis=0)
             totals[block, :] = total
-            return none
-
-        lax.fori_loop(0, size // count, some, 0)
+
+        if size % FIRST_ROWS:
+            some(pl.ds(start, size), size)
+        else:
+            def more(index, none):
+                some(pl.ds(pl.multiple_of(start + index * FIRST_ROWS, RELAY_ROWS), FIRST_ROWS), FIRST_ROWS)
+                return none
+
+            lax.fori_loop(0, size // FIRST_ROWS, more, 0)
 
     def finish(chunk, none):
         block = rows_of(chunk)
@@ -360,17 +374,17 @@
     part().start()
     meet(0)
 
-    def pass_on(group, count):
-        if count:
+    def pass_on(group, blocks):
+        if sum(blocks):
             with jax.named_scope("w_relay"):
-                relay_all(group, count).wait_recv()
-            for index in range(count):
-                for parity in range(2):
-                    for cross in range(2):
+                relay_all(group, sum(blocks) // 2).wait_recv()
+            for parity in range(2):
+                for cross in range(2):
+                    for index in range(blocks[parity ^ cross]):
                         from_relay(group, index, parity, cross).start()
 
-    for group in range(2):
-        for_count(relays[group], functools.partial(pass_on, group))
+    for team in range(2):
+        for_kind(relays[team], functools.partial(pass_on, team))
     for turn in range(1, n_aa - 1):
         meet(turn)
     with jax.named_scope("w_part"):
@@ -385,25 +399,28 @@
             first(step, slot[step], 0, rows)
             send_late(step, slot[step])
 
-    def take_group(group, count):
+    def land_group(group, blocks):
+        count = sum(blocks) // 2
         if count:
             with jax.named_scope("w_corner"):
                 landed(corner_recv.at[group], pl.ds(2, half), relay_block(0, count)).wait_recv()
-            for step, place in groups[group]:
-                first(step, place, rows - count * RELAY_ROWS, count * RELAY_ROWS)
         with jax.named_scope("w_last"):
             landed(last_recv.at[axes[group]], pl.ds(2, half), pl.ds(*last(count))).wait_recv()
-        for cross in (0, 1):
-            step, place = groups[group][cross]
-            first(step, place, *last(count))
+
+    def take_group(group):
+        for_kind(fed[group], functools.partial(land_group, group))
+        for turn in range(2):
+            cross = lax.rem(ba + turn, 2)
+            step, place = groups[group][0][0] + cross, groups[group][0][1] + half * cross
+            first(step, place, EARLY_ROWS, rows - EARLY_ROWS)
             send_late(step, place)
 
     pl.when(jnp.logical_not(beside))(take_diagonal)
     take_early(0)
-    for_count(fed[0], functools.partial(take_group, 0))
+    take_group(0)
     pl.when(beside)(take_diagonal)
     take_early(1)
-    for_count(fed[1], functools.partial(take_group, 1))
+    take_group(1)
     with jax.named_scope("finish"):
         lax.fori_loop(0, chunks, finish, 0)
     with jax.named_scope("w_tail"):
@@ -415,12 +432,13 @@
     with jax.named_scope("w_last_sends"):
         landed(sibling_recv, everything).wait_send()
 
-        def wait_relay(group, count):
-            if count:
-                relay_all(group, count).wait_send()
-
-        for group in range(2):
-            for_count(relays[group], functools.partial(wait_relay, group))
+        def wait_relay(group, blocks):
+            if sum(blocks):
+                relay_all(group, sum(blocks) // 2).wait_send()
+
+        for team in range(2):
+            for_kind(relays[team], functools.partial(wait_relay, team))
+
         remote_copy(tails, tails, small_send, tail_recv, {"ba": ba ^ 1}).wait_send()
 
 
@@ -476,7 +494,7 @@
             pltpu.SemaphoreType.DMA,
             pltpu.SemaphoreType.REGULAR,
             pltpu.SemaphoreType.REGULAR((n_aa - 1,)),
-            pltpu.VMEM((2, 2, 2, 2, RELAY_ROWS, width), jnp.bfloat16),
+            pltpu.VMEM((2, 3, 2, 2, RELAY_ROWS, width), jnp.bfloat16),
             pltpu.SemaphoreType.DMA((2,)),
             pltpu.SemaphoreType.DMA((2,)),
             pltpu.SemaphoreType.DMA((2,)),

time: 22.1 us -> 22.1 us (level)
  no operation moved by 1% of the time
where the time goes in v5:
time: 22.1 us; the launch traced here: 21.9 us
  Pallas kernels  21.3 us (96%)
  between operations  0.64 us (3%)
    pallas_call x1, Pallas kernels, fused(): pl.pallas_call(functools.partial(kernel, n_ba, n_aa), out_shape=(pltpu.VM...  20.3 us
    pallas_call x1, Pallas kernels, fused(): pl.pallas_call(store, out_shape=(jax.ShapeDtypeStruct((rows, depth), jnp....  0.98 us

profile of v5, /device:TPU:0, one launch (start us, length us, event | category | flops | bytes accessed | tf_op | source)
XLA Modules:
  0.0 21.9 jit_solution(16712169307772096579)
XLA Ops:
  0.6 20.3 %regroup_backward.1 = (bf16[128,4096]{1,0:T(8,128)(2,1)S(1)}, f32[1,512]{1,0:T(1,128)S(1)}) custom-call(bf16[1024,512]{1,0:T(8,128)(2,1)} %grad_hbm.1, bf16[128,4096]{1,0:T(8,128)(2,1)} %input_hbm.1, s32[128,128]{1,0:T(8,128)} %bits_hbm.1, f32[1,4096]{1,0:T(1,128)} %bitcast.2), custom_call_target="tpu_custom_call" | custom-call | tf_op jit(solution)/shard_map/regroup_backward/pallas_call | solution.py:463
  21.0 1.0 %store_results.1 = (bf16[128,4096]{1,0:T(8,128)(2,1)}, f32[1,512]{1,0:T(1,128)}) custom-call(bf16[128,4096]{1,0:T(8,128)(2,1)S(1)} %get-tuple-element.6.grad_vmem, f32[1,512]{1,0:T(1,128)S(1)} %get-tuple-element.7.share_vmem), custom_call_target="tpu_custom_call" | custom-call | tf_op jit(solution)/shard_map/store_results/pallas_call | solution.py:505

commit v6 on v5

--- a/solution.py
+++ b/solution.py
@@ -165,18 +165,18 @@
         group = 1 - swapped if axis_of(step) else swapped
         return remote_copy(
             staged.at[slot[step], relay_block(index)], relayed.at[group, index, parity, step % 2],
-            send_sem, relay_recv.at[group], {"aa": mirror, "ba": target + 1 - parity},
+            send_sem, relay_recv, {"aa": mirror, "ba": target + 1 - parity},
         )
 
     def from_relay(group, index, parity, cross):
         return remote_copy(
             relayed.at[group, index, parity, cross], arrived.at[groups[group][cross][1], relay_block(index)],
-            relay_send.at[group], corner_recv.at[group], {"aa": mirror, "ba": ba - 1 + parity},
+            relay_send, corner_recv.at[group], {"aa": mirror, "ba": ba - 1 + parity},
         )
 
-    def relay_all(group, count):
-        blocks = relayed.at[group, pl.ds(0, count)]
-        return remote_copy(blocks, blocks, relay_send.at[group], relay_recv.at[group], {"ba": ba ^ 1})
+    def relay_all(count):
+        blocks = relayed.at[0, pl.ds(0, count)] if count < 3 else relayed.at[0]
+        return remote_copy(blocks, blocks, relay_send, relay_recv, {"ba": ba ^ 1})
 
     def landed(recv, *at):
         return remote_copy(staged.at[at], arrived.at[at], send_sem, recv, {"ba": ba ^ 1})
@@ -374,17 +374,25 @@
     part().start()
     meet(0)
 
-    def pass_on(group, blocks):
-        if sum(blocks):
-            with jax.named_scope("w_relay"):
-                relay_all(group, sum(blocks) // 2).wait_recv()
+    others_relayed = RELAYED[2]
+
+    def both_groups(kind):
+        return (RELAYED[kind], (0, 0) if kind == 1 else others_relayed)
+
+    def relay_total(kind):
+        return sum(sum(blocks) for blocks in both_groups(kind)) // 2
+
+    def pass_on(kind):
+        with jax.named_scope("w_relay"):
+            relay_all(relay_total(kind)).wait_recv()
+        for group, blocks in enumerate(both_groups(kind)):
             for parity in range(2):
                 for cross in range(2):
                     for index in range(blocks[parity ^ cross]):
                         from_relay(group, index, parity, cross).start()
 
-    for team in range(2):
-        for_kind(relays[team], functools.partial(pass_on, team))
+    for kind, flag in enumerate(relays[0]):
+        pl.when(flag)(functools.partial(pass_on, kind))
     for turn in range(1, n_aa - 1):
         meet(turn)
     with jax.named_scope("w_part"):
@@ -432,12 +440,10 @@
     with jax.named_scope("w_last_sends"):
         landed(sibling_recv, everything).wait_send()
 
-        def wait_relay(group, blocks):
-            if sum(blocks):
-                relay_all(group, sum(blocks) // 2).wait_send()
-
-        for team in range(2):
-            for_kind(relays[team], functools.partial(wait_relay, team))
+        for kind, flag in enumerate(relays[0]):
+            @pl.when(flag)
+            def _(kind=kind):
+                relay_all(relay_total(kind)).wait_send()
 
         remote_copy(tails, tails, small_send, tail_recv, {"ba": ba ^ 1}).wait_send()
 
@@ -495,8 +501,8 @@
             pltpu.SemaphoreType.REGULAR,
             pltpu.SemaphoreType.REGULAR((n_aa - 1,)),
             pltpu.VMEM((2, 3, 2, 2, RELAY_ROWS, width), jnp.bfloat16),
-            pltpu.SemaphoreType.DMA((2,)),
-            pltpu.SemaphoreType.DMA((2,)),
+            pltpu.SemaphoreType.DMA,
+            pltpu.SemaphoreType.DMA,
             pltpu.SemaphoreType.DMA((2,)),
         ],
         compiler_params=pltpu.CompilerParams(collective_id=0, has_side_effects=True),

time: 22.1 us -> 22.1 us (level)
  no operation moved by 1% of the time
where the time goes in v6:
time: 22.1 us; the launch traced here: 21.9 us
  Pallas kernels  21.3 us (96%)
  between operations  0.64 us (3%)
    pallas_call x1, Pallas kernels, fused(): pl.pallas_call(functools.partial(kernel, n_ba, n_aa), out_shape=(pltpu.VM...  20.3 us
    pallas_call x1, Pallas kernels, fused(): pl.pallas_call(store, out_shape=(jax.ShapeDtypeStruct((rows, depth), jnp....  0.98 us

profile of v6, /device:TPU:0, one launch (start us, length us, event | category | flops | bytes accessed | tf_op | source)
XLA Modules:
  0.0 21.9 jit_solution(15317106447970707770)
XLA Ops:
  0.6 20.3 %regroup_backward.1 = (bf16[128,4096]{1,0:T(8,128)(2,1)S(1)}, f32[1,512]{1,0:T(1,128)S(1)}) custom-call(bf16[1024,512]{1,0:T(8,128)(2,1)} %grad_hbm.1, bf16[128,4096]{1,0:T(8,128)(2,1)} %input_hbm.1, s32[128,128]{1,0:T(8,128)} %bits_hbm.1, f32[1,4096]{1,0:T(1,128)} %bitcast.2), custom_call_target="tpu_custom_call" | custom-call | tf_op jit(solution)/shard_map/regroup_backward/pallas_call | solution.py:469
  20.9 1.0 %store_results.1 = (bf16[128,4096]{1,0:T(8,128)(2,1)}, f32[1,512]{1,0:T(1,128)}) custom-call(bf16[128,4096]{1,0:T(8,128)(2,1)S(1)} %get-tuple-element.6.grad_vmem, f32[1,512]{1,0:T(1,128)S(1)} %get-tuple-element.7.share_vmem), custom_call_target="tpu_custom_call" | custom-call | tf_op jit(solution)/shard_map/store_results/pallas_call | solution.py:511
